TPU v7x, 32 devices: a whole 2x2x4 slice. The times are simulated.
32 devices in a mesh: section: 2 (over x), expert: 4 (over y, core), dp: 4 (over z).
Axes of the slice: x: 2, y: 2, z: 4, core: 2. Of those that a mesh axis runs over, the one named last changes fastest.
Arguments:
- arrivals: bfloat16 [2, 1024, 2048], P('section', ('expert', 'dp')), may hold values from -6 to 6
- fresh: bfloat16 [1, 1024, 2048], P(None, ('expert', 'dp')), may hold values from -6 to 6
- routes: int32 [2, 2, 1024, 6], P('section', None, ('expert', 'dp')), may hold values from 0 to 63, as said below
- gates: bfloat16 [2, 2, 1024, 6], P('section', None, ('expert', 'dp')), may hold values from 0.099609375 to 1
- cotangent: bfloat16 [2, 2, 1024, 2048], P('section', None, ('expert', 'dp')), may hold values from -0.3125 to 0.3125
- norm_gain: float32 [2, 2048], P('section'), may hold values from 0.5 to 1.5
- w_gate: bfloat16 [2, 1408, 2048], P('section', 'expert', 'dp'), may hold values from -0.125 to 0.125
- w_up: bfloat16 [2, 1408, 2048], P('section', 'expert', 'dp'), may hold values from -0.125 to 0.125
- w_down: bfloat16 [2, 1408, 2048], P('section', 'expert', 'dp'), may hold values from -0.15625 to 0.15625
Outputs:
- layer_out: bfloat16 [2, 2, 1024, 2048], P('section', None, ('expert', 'dp'))
- grad_down: float32 [2, 1408, 2048], P('section', 'expert', 'dp')
Inputs may be any that keep to these rules, and one draw needn't show every extreme that they name: `routes`: each token's 6 entries are different expert numbers.
All inputs are finite; a program needn't handle non-finite values.
Results may differ from a plain program's by a relative error of at most 0.0085.
Values may be sent and summed in bfloat16 or wider, within the bound.
A program may use at most 64 MiB of HBM per device.

v0:
```python
import jax
import jax.numpy as jnp
from jax import lax
from jax.sharding import PartitionSpec as P

SPLIT = 4
CAP = 12


def shifted_2(shard, axis, by):
    count = lax.axis_size(axis)
    pairs = [(i, i + by) for i in range(count) if 0 <= i + by < count]
    return lax.ppermute(shard, axis, pairs)


def local(arrivals, fresh, routes, gates, cotangent, norm_gain, w_gate, w_up, w_down):
    n_expert = lax.axis_size("expert")
    flight = n_expert // SPLIT
    section_index = lax.axis_index("section")
    tok_rows = arrivals.shape[1]
    model_width = arrivals.shape[2]
    step_count = routes.shape[1]
    gains = norm_gain[0]
    gate_local, up_local, down_local = (
        lax.all_gather(w_gate[0], "dp", axis=1, tiled=True),
        lax.all_gather(w_up[0], "dp", axis=1, tiled=True),
        lax.all_gather(w_down[0], "dp", axis=1, tiled=True),
    )
    hid_rows = gate_local.shape[0]
    slot_ids = jnp.arange(CAP, dtype=jnp.int32)
    expert_ids = jnp.arange(flight, dtype=jnp.int32)
    highest = lax.Precision.HIGHEST
    row_dims = (((0,), (0,)), ((), ()))

    def selection(step_index):
        routing = routes[0, step_index]
        weights = gates[0, step_index].astype(jnp.float32)
        matches = routing[:, :, None] == expert_ids[None, None, :]
        naming = jnp.any(matches, axis=1).astype(jnp.int32)
        shares = jnp.sum(jnp.where(matches, weights[:, :, None], 0.0), axis=1)
        places = jnp.cumsum(naming, axis=0) - naming
        chosen = (naming.T[:, None, :] == 1) & (places.T[:, None, :] == slot_ids[None, :, None])
        select = chosen.reshape(flight * CAP, tok_rows).astype(jnp.bfloat16)
        slot_gate = jnp.sum(jnp.where(chosen, shares.T[:, None, :], 0.0), axis=2).reshape(
            flight * CAP
        )
        counts = jnp.minimum(jnp.sum(naming, axis=0), CAP)
        return (select, slot_gate, counts)

    def fan_out(block_in):
        spread = jnp.broadcast_to(block_in[:, None], (flight, SPLIT) + block_in.shape[1:])
        return spread.reshape((n_expert,) + block_in.shape[1:])

    def pack_rows(select, values):
        rows = jnp.dot(select, values, preferred_element_type=jnp.float32).astype(jnp.bfloat16)
        return fan_out(rows.reshape(flight, CAP, model_width))

    picks = [selection(turn_num) for turn_num in range(step_count)]
    incoming = arrivals[0]
    grad_total = jnp.zeros((hid_rows, model_width), jnp.float32)
    outputs = []
    for turn_num in range(step_count):
        if turn_num > 0:
            shifted = shifted_2(outputs[-1], "section", 1)
            incoming = jnp.where(section_index == 0, fresh[turn_num - 1], shifted)
        floats = incoming.astype(jnp.float32)
        scale = lax.rsqrt(jnp.mean(floats * floats, axis=1, keepdims=True) + 0.5)
        normed = (floats * scale * gains[None, :]).astype(jnp.bfloat16)
        select, slot_gate, counts = picks[turn_num]
        send_tok = pack_rows(select, normed)
        send_cot = pack_rows(select, cotangent[0, turn_num])
        send_gate = fan_out(slot_gate.reshape(flight, CAP).astype(jnp.bfloat16))
        send_count = fan_out(counts)
        rows_tok, rows_cot, rows_gate, rows_count = (
            lax.all_to_all(send_tok, "expert", split_axis=0, concat_axis=0, tiled=True),
            lax.all_to_all(send_cot, "expert", split_axis=0, concat_axis=0, tiled=True),
            lax.all_to_all(send_gate, "expert", split_axis=0, concat_axis=0, tiled=True),
            lax.all_to_all(send_count, "expert", split_axis=0, concat_axis=0, tiled=True),
        )
        total_rows = n_expert * CAP
        flat_tok = rows_tok.reshape(total_rows, model_width)
        flat_cot = rows_cot.reshape(total_rows, model_width)
        flat_gate = rows_gate.reshape(total_rows)
        dims = (((1,), (1,)), ((), ()))
        gate_act = lax.dot_general(flat_tok, gate_local, dims, preferred_element_type=jnp.float32)
        up_act = lax.dot_general(flat_tok, up_local, dims, preferred_element_type=jnp.float32)
        hidden = (jax.nn.silu(gate_act) * up_act).astype(jnp.bfloat16)
        partial_value = jnp.dot(hidden, down_local, preferred_element_type=jnp.float32).astype(
            jnp.bfloat16
        )
        weighted = (hidden.astype(jnp.float32) * flat_gate.astype(jnp.float32)[:, None]).astype(
            jnp.bfloat16
        )
        expert_partial_value = partial_value
        grad_add = lax.dot_general(weighted, flat_cot, row_dims, preferred_element_type=jnp.float32)
        partial_value, grad_add = (
            expert_partial_value.reshape(n_expert, CAP, model_width),
            grad_add,
        )
        returned = lax.all_to_all(partial_value, "expert", split_axis=0, concat_axis=0, tiled=True)
        expert_out = jnp.sum(
            returned.reshape(flight, SPLIT, CAP, model_width).astype(jnp.float32), axis=1
        ).reshape(flight * CAP, model_width)
        mixing = select.astype(jnp.float32).T * slot_gate[None, :]
        mixture = jnp.dot(mixing, expert_out, precision=highest)
        result = (floats + mixture).astype(jnp.bfloat16)
        outputs.append(result)
        grad_total = grad_total + grad_add
    grad_part = lax.psum_scatter(grad_total, "dp", scatter_dimension=1, tiled=True)
    return (jnp.stack(outputs)[None], grad_part[None])


def solution(mesh):
    placed = (
        P("section", ("expert", "dp"), None),
        P(None, ("expert", "dp"), None),
        P("section", None, ("expert", "dp"), None),
        P("section", None, ("expert", "dp"), None),
        P("section", None, ("expert", "dp"), None),
        P("section", None),
        P("section", "expert", "dp"),
        P("section", "expert", "dp"),
        P("section", "expert", "dp"),
    )
    return jax.shard_map(
        local,
        mesh=mesh,
        in_specs=placed,
        out_specs=(P("section", None, ("expert", "dp"), None), P("section", "expert", "dp")),
        check_vma=False,
    )
```

profile of v0, /device:TPU:0, one launch (start us, length us, event | category | flops | bytes accessed | tf_op | source)
XLA Modules:
  0.0 242.2 jit_solution(11923948752257591277)
XLA Ops:
  9.4 0.8 compare_reduce_fusion
  10.5 1.1 fusion.26
  11.9 0.7 reshape.550
  12.7 4.3 %all-to-all-start = ((bf16[4,12,2048]{2,1,0:T(8,128)(2,1)}), bf16[4,12,2048]{2,1,0:T(8,128)(2,1)S(1)}, u32[]{:S(2)}, u32[]{:S(2)}) async-start(bf16[4,12,2048]{2,1,0:T(8,128)(2,1)} %reshape.550), calls=%async_computation | async-start | bytes 524288 | tf_op jit(solution)/shard_map/all_to_all | solution.py:75
  17.7 5.3 %all-to-all-done = bf16[4,12,2048]{2,1,0:T(8,128)(2,1)S(1)} async-done(((bf16[4,12,2048]{2,1,0:T(8,128)(2,1)}), bf16[4,12,2048]{2,1,0:T(8,128)(2,1)S(1)}, u32[]{:S(2)}, u32[]{:S(2)}) %all-to-all-start) | async-done | bytes 196640 | tf_op jit(solution)/shard_map/all_to_all | solution.py:75
  23.0 24.1 %all-gather.7.cloned.1.call-done = bf16[1,352,2048]{2,1,0:T(8,128)(2,1)} async-done(((bf16[1,352,512]{2,1,0:T(8,128)(2,1)}), bf16[1,352,2048]{2,1,0:T(8,128)(2,1)}) %all-gather.7.cloned.1.call-update) | async-done | bytes 1441808 | tf_op jit(solution)/shard_map/all_gather | solution.py:25
  47.0 1.9 fusion.11
  49.0 33.5 %all-gather.9.cloned.1.call-done = bf16[1,352,2048]{2,1,0:T(8,128)(2,1)} async-done(((bf16[1,352,512]{2,1,0:T(8,128)(2,1)}), bf16[1,352,2048]{2,1,0:T(8,128)(2,1)}) %all-gather.9.cloned.1.call-update) | async-done | bytes 1441808 | tf_op jit(solution)/shard_map/all_gather | solution.py:26
  82.5 1.9 fusion.22
  84.4 33.4 %all-gather.11.cloned.1.call-done = bf16[1,352,2048]{2,1,0:T(8,128)(2,1)} async-done(((bf16[1,352,512]{2,1,0:T(8,128)(2,1)}), bf16[1,352,2048]{2,1,0:T(8,128)(2,1)}) %all-gather.11.cloned.1.call-update) | async-done | bytes 1441808 | tf_op jit(solution)/shard_map/all_gather | solution.py:27
  117.8 1.7 convolution_convert_fusion.1
  119.6 0.8 reshape.552
  120.3 3.4 %all-to-all-start.1 = ((bf16[4,12,2048]{2,1,0:T(8,128)(2,1)}), bf16[4,12,2048]{2,1,0:T(8,128)(2,1)S(1)}, u32[]{:S(2)}, u32[]{:S(2)}) async-start(bf16[4,12,2048]{2,1,0:T(8,128)(2,1)} %reshape.552), calls=%async_computation.1 | async-start | bytes 524288 | tf_op jit(solution)/shard_map/all_to_all | solution.py:100
  123.9 5.8 %all-to-all-done.1 = bf16[4,12,2048]{2,1,0:T(8,128)(2,1)S(1)} async-done(((bf16[4,12,2048]{2,1,0:T(8,128)(2,1)}), bf16[4,12,2048]{2,1,0:T(8,128)(2,1)S(1)}, u32[]{:S(2)}, u32[]{:S(2)}) %all-to-all-start.1) | async-done | bytes 196640 | tf_op jit(solution)/shard_map/all_to_all | solution.py:100
  130.3 3.2 %all-to-all-start.4 = ((bf16[4,1,12]{2,1,0:T(2,128)(2,1)}), bf16[4,1,12]{2,1,0:T(2,128)(2,1)S(1)}, u32[]{:S(2)}, u32[]{:S(2)}) async-start(bf16[4,1,12]{2,1,0:T(2,128)(2,1)} %reshape.557), calls=%async_computation.4 | async-start | bytes 4096 | tf_op jit(solution)/shard_map/all_to_all | solution.py:77
  134.2 3.0 %all-to-all-done.4 = bf16[4,1,12]{2,1,0:T(2,128)(2,1)S(1)} async-done(((bf16[4,1,12]{2,1,0:T(2,128)(2,1)}), bf16[4,1,12]{2,1,0:T(2,128)(2,1)S(1)}, u32[]{:S(2)}, u32[]{:S(2)}) %all-to-all-start.4) | async-done | bytes 128 | tf_op jit(solution)/shard_map/all_to_all | solution.py:77
  137.8 3.2 %all-to-all-start.6 = ((bf16[4,1,12]{2,1,0:T(2,128)(2,1)}), bf16[4,1,12]{2,1,0:T(2,128)(2,1)S(1)}, u32[]{:S(2)}, u32[]{:S(2)}) async-start(bf16[4,1,12]{2,1,0:T(2,128)(2,1)} %reshape.560), calls=%async_computation.6 | async-start | bytes 4096 | tf_op jit(solution)/shard_map/all_to_all | solution.py:77
  141.0 3.5 %collective-permute-start = (bf16[64,2048]{1,0:T(8,128)(2,1)S(1)}, bf16[64,2048]{1,0:T(8,128)(2,1)S(1)}, u32[]{:S(2)}, u32[]{:S(2)}) collective-permute-start(bf16[64,2048]{1,0:T(8,128)(2,1)S(1)} %fusion), channel_id=1, source_target_pairs={{0,16},{1,17},{2,18},{3,19},{4,20},{5,21},{6,22},{7,23},{8,24},{9,... | collective-permute-start | bytes 786440 | tf_op jit(solution)/shard_map/ppermute | solution.py:13
  145.4 3.4 %all-to-all-start.5 = ((bf16[4,12,2048]{2,1,0:T(8,128)(2,1)}), bf16[4,12,2048]{2,1,0:T(8,128)(2,1)S(1)}, u32[]{:S(2)}, u32[]{:S(2)}) async-start(bf16[4,12,2048]{2,1,0:T(8,128)(2,1)} %reshape.558), calls=%async_computation.5 | async-start | bytes 524288 | tf_op jit(solution)/shard_map/all_to_all | solution.py:76
  149.0 5.8 %all-to-all-done.5 = bf16[4,12,2048]{2,1,0:T(8,128)(2,1)S(1)} async-done(((bf16[4,12,2048]{2,1,0:T(8,128)(2,1)}), bf16[4,12,2048]{2,1,0:T(8,128)(2,1)S(1)}, u32[]{:S(2)}, u32[]{:S(2)}) %all-to-all-start.5) | async-done | bytes 196640 | tf_op jit(solution)/shard_map/all_to_all | solution.py:76
  155.5 3.4 %all-to-all-start.7 = ((bf16[4,12,2048]{2,1,0:T(8,128)(2,1)}), bf16[4,12,2048]{2,1,0:T(8,128)(2,1)S(1)}, u32[]{:S(2)}, u32[]{:S(2)}) async-start(bf16[4,12,2048]{2,1,0:T(8,128)(2,1)} %reshape.561), calls=%async_computation.7 | async-start | bytes 524288 | tf_op jit(solution)/shard_map/all_to_all | solution.py:76
  159.8 5.1 %all-to-all-done.7 = bf16[4,12,2048]{2,1,0:T(8,128)(2,1)S(1)} async-done(((bf16[4,12,2048]{2,1,0:T(8,128)(2,1)}), bf16[4,12,2048]{2,1,0:T(8,128)(2,1)S(1)}, u32[]{:S(2)}, u32[]{:S(2)}) %all-to-all-start.7) | async-done | bytes 196640 | tf_op jit(solution)/shard_map/all_to_all | solution.py:76
  166.1 0.7 reshape.554
  166.8 3.4 %all-to-all-start.2 = ((bf16[4,12,2048]{2,1,0:T(8,128)(2,1)}), bf16[4,12,2048]{2,1,0:T(8,128)(2,1)S(1)}, u32[]{:S(2)}, u32[]{:S(2)}) async-start(bf16[4,12,2048]{2,1,0:T(8,128)(2,1)} %reshape.554), calls=%async_computation.2 | async-start | bytes 524288 | tf_op jit(solution)/shard_map/all_to_all | solution.py:75
  170.3 1.4 fusion.43
  171.7 4.5 %all-to-all-done.2 = bf16[4,12,2048]{2,1,0:T(8,128)(2,1)S(1)} async-done(((bf16[4,12,2048]{2,1,0:T(8,128)(2,1)}), bf16[4,12,2048]{2,1,0:T(8,128)(2,1)S(1)}, u32[]{:S(2)}, u32[]{:S(2)}) %all-to-all-start.2) | async-done | bytes 196640 | tf_op jit(solution)/shard_map/all_to_all | solution.py:75
  176.3 2.0 fusion.9
  178.9 2.2 convolution_add_fusion
  181.2 1.3 copy-done
  182.9 8.4 %all_to_all.42 = bf16[4,12,2048]{2,1,0:T(8,128)(2,1)S(1)} all-to-all(bf16[4,12,2048]{2,1,0:T(8,128)(2,1)S(1)} %reshape.556), channel_id=1, replica_groups=mesh['section'=2,'expert'=4,'dp'=4] {'expert'}, dimensions={0} | all-to-all | bytes 393216 | tf_op jit(solution)/shard_map/all_to_all | solution.py:100
  192.0 0.8 maximum_bitcast_fusion
  192.9 42.8 %reduce-scatter.2.cloned.1.call-done = f32[352,512]{1,0:T(8,128)} async-done(((f32[352,2048]{1,0:T(8,128)}), f32[352,512]{1,0:T(8,128)}) %reduce-scatter.2.cloned.1.call-update) | async-done | bytes 720912 | tf_op jit(solution)/shard_map/reduce_scatter | solution.py:109
  (78 shorter events, 11.0 us)
Async XLA Ops:
  7.2 10.1 %copy-start.10 = (s32[1,2,64,6]{2,1,3,0:T(2,128)S(1)}, s32[1,2,64,6]{2,1,3,0:T(2,128)}, u32[]{:S(2)}) copy-start(s32[1,2,64,6]{2,1,3,0:T(2,128)} %param.11) | copy-start | bytes 9220
  7.2 4.5 %copy-start.2 = (bf16[1,64,2048]{2,1,0:T(8,128)(2,1)S(1)}, bf16[1,64,2048]{2,1,0:T(8,128)(2,1)}, u32[]{:S(2)}) copy-start(bf16[1,64,2048]{2,1,0:T(8,128)(2,1)} %param.9) | copy-start | bytes 786436
  7.2 4.5 %copy-start.13 = (f32[1,2048]{1,0:T(1,128)S(1)}, f32[1,2048]{1,0:T(1,128)}, u32[]{:S(2)}) copy-start(f32[1,2048]{1,0:T(1,128)} %param.14) | copy-start | bytes 24580
  7.2 10.1 %copy-start.11 = (bf16[1,2,64,6]{2,1,3,0:T(2,128)(2,1)S(1)}, bf16[1,2,64,6]{2,1,3,0:T(2,128)(2,1)}, u32[]{:S(2)}) copy-start(bf16[1,2,64,6]{2,1,3,0:T(2,128)(2,1)} %param.12) | copy-start | bytes 4612
  7.2 39.8 %all-gather.7.cloned.1.call-start = ((), (), s32[]{:S(2)}) async-start(), calls=%async_computation.10 | async-start | bytes 1802240 | tf_op jit(solution)/shard_map/all_gather | solution.py:25
  7.9 74.5 %all-gather.9.cloned.1.call-start = ((), (), s32[]{:S(2)}) async-start(), calls=%async_computation.11 | async-start | bytes 1802240 | tf_op jit(solution)/shard_map/all_gather | solution.py:26
  8.7 109.1 %all-gather.11.cloned.1.call-start = ((), (), s32[]{:S(2)}) async-start(), calls=%async_computation.12 | async-start | bytes 1802240 | tf_op jit(solution)/shard_map/all_gather | solution.py:27
  12.7 10.3 %all-to-all-start = ((bf16[4,12,2048]{2,1,0:T(8,128)(2,1)}), bf16[4,12,2048]{2,1,0:T(8,128)(2,1)S(1)}, u32[]{:S(2)}, u32[]{:S(2)}) async-start(bf16[4,12,2048]{2,1,0:T(8,128)(2,1)} %reshape.550), calls=%async_computation | async-start | bytes 524288 | tf_op jit(solution)/shard_map/all_to_all | solution.py:75
  84.4 35.9 %copy-start.8 = (bf16[48,352]{1,0:T(8,128)(2,1)}, bf16[48,352]{1,0:T(8,128)(2,1)S(1)}, u32[]{:S(2)}) copy-start(bf16[48,352]{1,0:T(8,128)(2,1)S(1)} %fusion.22) | copy-start | bytes 101380
  84.4 39.3 %copy-start.7 = (bf16[1,2,64,2048]{3,2,1,0:T(8,128)(2,1)S(1)}, bf16[1,2,64,2048]{3,2,1,0:T(8,128)(2,1)}, u32[]{:S(2)}) copy-start(bf16[1,2,64,2048]{3,2,1,0:T(8,128)(2,1)} %param.13) | copy-start | bytes 1572868
  120.3 9.4 %all-to-all-start.1 = ((bf16[4,12,2048]{2,1,0:T(8,128)(2,1)}), bf16[4,12,2048]{2,1,0:T(8,128)(2,1)S(1)}, u32[]{:S(2)}, u32[]{:S(2)}) async-start(bf16[4,12,2048]{2,1,0:T(8,128)(2,1)} %reshape.552), calls=%async_computation.1 | async-start | bytes 524288 | tf_op jit(solution)/shard_map/all_to_all | solution.py:100
  130.3 6.9 %all-to-all-start.4 = ((bf16[4,1,12]{2,1,0:T(2,128)(2,1)}), bf16[4,1,12]{2,1,0:T(2,128)(2,1)S(1)}, u32[]{:S(2)}, u32[]{:S(2)}) async-start(bf16[4,1,12]{2,1,0:T(2,128)(2,1)} %reshape.557), calls=%async_computation.4 | async-start | bytes 4096 | tf_op jit(solution)/shard_map/all_to_all | solution.py:77
  134.2 30.7 %copy-start.5 = (bf16[64,2048]{1,0:T(8,128)(2,1)}, bf16[64,2048]{1,0:T(8,128)(2,1)S(1)}, u32[]{:S(2)}) copy-start(bf16[64,2048]{1,0:T(8,128)(2,1)S(1)} %fusion) | copy-start | bytes 786436
  137.8 6.9 %all-to-all-start.6 = ((bf16[4,1,12]{2,1,0:T(2,128)(2,1)}), bf16[4,1,12]{2,1,0:T(2,128)(2,1)S(1)}, u32[]{:S(2)}, u32[]{:S(2)}) async-start(bf16[4,1,12]{2,1,0:T(2,128)(2,1)} %reshape.560), calls=%async_computation.6 | async-start | bytes 4096 | tf_op jit(solution)/shard_map/all_to_all | solution.py:77
  141.0 24.0 %copy-start.9 = (bf16[1,64,2048]{2,1,0:T(8,128)(2,1)S(1)}, bf16[1,64,2048]{2,1,0:T(8,128)(2,1)}, u32[]{:S(2)}) copy-start(bf16[1,64,2048]{2,1,0:T(8,128)(2,1)} %param.10) | copy-start | bytes 786436
  141.0 23.9 %collective-permute-start = (bf16[64,2048]{1,0:T(8,128)(2,1)S(1)}, bf16[64,2048]{1,0:T(8,128)(2,1)S(1)}, u32[]{:S(2)}, u32[]{:S(2)}) collective-permute-start(bf16[64,2048]{1,0:T(8,128)(2,1)S(1)} %fusion), channel_id=1, source_target_pairs={{0,16},{1,17},{2,18},{3,19},{4,20},{5,21},{6,22},{7,23},{8,24},{9,... | collective-permute-start | bytes 786440 | tf_op jit(solution)/shard_map/ppermute | solution.py:13
  145.4 9.4 %all-to-all-start.5 = ((bf16[4,12,2048]{2,1,0:T(8,128)(2,1)}), bf16[4,12,2048]{2,1,0:T(8,128)(2,1)S(1)}, u32[]{:S(2)}, u32[]{:S(2)}) async-start(bf16[4,12,2048]{2,1,0:T(8,128)(2,1)} %reshape.558), calls=%async_computation.5 | async-start | bytes 524288 | tf_op jit(solution)/shard_map/all_to_all | solution.py:76
  155.5 9.4 %all-to-all-start.7 = ((bf16[4,12,2048]{2,1,0:T(8,128)(2,1)}), bf16[4,12,2048]{2,1,0:T(8,128)(2,1)S(1)}, u32[]{:S(2)}, u32[]{:S(2)}) async-start(bf16[4,12,2048]{2,1,0:T(8,128)(2,1)} %reshape.561), calls=%async_computation.7 | async-start | bytes 524288 | tf_op jit(solution)/shard_map/all_to_all | solution.py:76
  165.2 0.7 copy-start.3
  166.8 9.4 %all-to-all-start.2 = ((bf16[4,12,2048]{2,1,0:T(8,128)(2,1)}), bf16[4,12,2048]{2,1,0:T(8,128)(2,1)S(1)}, u32[]{:S(2)}, u32[]{:S(2)}) async-start(bf16[4,12,2048]{2,1,0:T(8,128)(2,1)} %reshape.554), calls=%async_computation.2 | async-start | bytes 524288 | tf_op jit(solution)/shard_map/all_to_all | solution.py:75
  170.3 65.5 %reduce-scatter.2.cloned.1.call-start = ((), (), s32[]{:S(2)}) async-start(), calls=%async_computation.9 | async-start | bytes 3604480 | tf_op jit(solution)/shard_map/reduce_scatter | solution.py:109
  176.3 2.1 copy-start.1
  176.3 2.6 %copy-start.12 = (f32[48]{0:T(128)S(1)}, f32[48]{0:T(128)}, u32[]{:S(2)}) copy-start(f32[48]{0:T(128)} %reshape.567) | copy-start | bytes 580
  181.1 1.4 copy-start
  182.5 8.9 %copy-start.4 = (bf16[64,2048]{1,0:T(8,128)(2,1)S(1)}, bf16[64,2048]{1,0:T(8,128)(2,1)}, u32[]{:S(2)}) copy-start(bf16[64,2048]{1,0:T(8,128)(2,1)} %copy-done.3) | copy-start | bytes 786436
  182.5 9.5 %copy-start.6 = (bf16[64,2048]{1,0:T(8,128)(2,1)S(1)}, bf16[64,2048]{1,0:T(8,128)(2,1)}, u32[]{:S(2)}) copy-start(bf16[64,2048]{1,0:T(8,128)(2,1)} %copy-done.5) | copy-start | bytes 786436
Sparse Core Ops, SparseCore 0:
  9.6 37.4 all-gather.6
  48.6 33.8 all-gather.8
  84.0 33.7 all-gather.10
  181.3 54.3 reduce-scatter.1
where the time goes:
time: 243 us; the launch traced here: 242 us
  waiting for transfers between devices  166 us (68%)
  starting transfers between devices  28 us (12%)
  matrix products  14.2 us (6%)
  between operations  14.2 us (6%)
  blocking collectives  8.39 us (3%)
  local copies, waits for them, and re-layouts  8.09 us (3%)
  other arithmetic  3.92 us (2%)
    reduce_scatter x1, waiting for transfers between devices, local(): lax.psum_scatter(grad_total, 'dp', scatter_dimension=1, tiled=True)  42.8 us
    all_gather x1, waiting for transfers between devices, local(): lax.all_gather(w_up[0], 'dp', axis=1, tiled=True)  33.5 us
    all_gather x1, waiting for transfers between devices, local(): lax.all_gather(w_down[0], 'dp', axis=1, tiled=True)  33.4 us
    all_gather x1, waiting for transfers between devices, local(): lax.all_gather(w_gate[0], 'dp', axis=1, tiled=True)  24.1 us
    all_to_all x2, waiting for transfers between devices, local(): lax.all_to_all(send_cot, 'expert', split_axis=0, concat_axis=0, tiled=True)  10.9 us
    all_to_all x2, waiting for transfers between devices, local(): lax.all_to_all(send_tok, 'expert', split_axis=0, concat_axis=0, tiled=True)  9.79 us
    all_to_all x1, blocking collectives, local(): lax.all_to_all(partial_value, 'expert', split_axis=0, concat_axis=0, tile...  8.39 us
    all_to_all x2, starting transfers between devices, local(): lax.all_to_all(send_tok, 'expert', split_axis=0, concat_axis=0, tiled=True)  7.67 us
  transfers between devices with their start and end apart: 12, of which 11 were waited for; matrix products, arithmetic and copies ran while one was open for 6% of the time, Pallas kernels for 0%

commit v1 on v0

--- a/solution.py
+++ b/solution.py
@@ -22,7 +22,7 @@
     step_count = routes.shape[1]
     gains = norm_gain[0]
     gate_local, up_local, down_local = (
-        lax.all_gather(w_gate[0], "dp", axis=1, tiled=True),
+        jnp.concatenate(lax.all_gather(w_gate[0], "dp"), axis=1),
         lax.all_gather(w_up[0], "dp", axis=1, tiled=True),
         lax.all_gather(w_down[0], "dp", axis=1, tiled=True),
     )

time: 243 us -> 243 us (level)
    dot_general x2, matrix products: 3.95 us -> 1.12 us  [local(): lax.dot_general(flat_tok, gate_local, dims, preferred_element_type=jnp.fl...]
  transfers between devices with their start and end apart: 12 -> 12, of which waited for: 11 -> 10; matrix products, arithmetic and copies ran while one was open for 6% -> 7% of each run, Pallas kernels for 0% -> 0%
where the time goes in v1:
time: 243 us; the launch traced here: 242 us
  waiting for transfers between devices  164 us (67%)
  starting transfers between devices  28.7 us (12%)
  between operations  14.2 us (6%)
  matrix products  13 us (5%)
  local copies, waits for them, and re-layouts  10.2 us (4%)
  blocking collectives  8.39 us (3%)
  other arithmetic  3.92 us (2%)
    reduce_scatter x1, waiting for transfers between devices, local(): lax.psum_scatter(grad_total, 'dp', scatter_dimension=1, tiled=True)  43.3 us
    all_gather x1, waiting for transfers between devices, local(): lax.all_gather(w_down[0], 'dp', axis=1, tiled=True)  33.4 us
    all_gather x1, waiting for transfers between devices, local(): lax.all_gather(w_up[0], 'dp', axis=1, tiled=True)  33.3 us
    all_gather x1, waiting for transfers between devices, local(): lax.all_gather(w_gate[0], 'dp')  24 us
    all_to_all x2, waiting for transfers between devices, local(): lax.all_to_all(send_cot, 'expert', split_axis=0, concat_axis=0, tiled=True)  11 us
    all_to_all x1, blocking collectives, local(): lax.all_to_all(partial_value, 'expert', split_axis=0, concat_axis=0, tile...  8.39 us
    all_to_all x2, waiting for transfers between devices, local(): lax.all_to_all(send_tok, 'expert', split_axis=0, concat_axis=0, tiled=True)  8.09 us
    all_to_all x2, starting transfers between devices, local(): lax.all_to_all(send_tok, 'expert', split_axis=0, concat_axis=0, tiled=True)  7.67 us
  transfers between devices with their start and end apart: 12, of which 10 were waited for; matrix products, arithmetic and copies ran while one was open for 7% of the time, Pallas kernels for 0%

profile of v1, /device:TPU:0, one launch (start us, length us, event | category | flops | bytes accessed | tf_op | source)
XLA Modules:
  0.0 242.4 jit_solution(18441407254007996395)
XLA Ops:
  9.4 0.8 compare_reduce_fusion
  10.5 1.1 fusion.22
  11.9 0.7 reshape.556
  12.7 4.3 %all-to-all-start = ((bf16[4,12,2048]{2,1,0:T(8,128)(2,1)}), bf16[4,12,2048]{2,1,0:T(8,128)(2,1)S(1)}, u32[]{:S(2)}, u32[]{:S(2)}) async-start(bf16[4,12,2048]{2,1,0:T(8,128)(2,1)} %reshape.556), calls=%async_computation | async-start | bytes 524288 | tf_op jit(solution)/shard_map/all_to_all | solution.py:75
  17.7 5.3 %all-to-all-done = bf16[4,12,2048]{2,1,0:T(8,128)(2,1)S(1)} async-done(((bf16[4,12,2048]{2,1,0:T(8,128)(2,1)}), bf16[4,12,2048]{2,1,0:T(8,128)(2,1)S(1)}, u32[]{:S(2)}, u32[]{:S(2)}) %all-to-all-start) | async-done | bytes 196640 | tf_op jit(solution)/shard_map/all_to_all | solution.py:75
  23.0 24.0 %all-gather.6.cloned.1.call-done = bf16[4,352,512]{2,1,0:T(8,128)(2,1)} async-done(((bf16[1,352,512]{2,1,0:T(8,128)(2,1)}), bf16[4,352,512]{2,1,0:T(8,128)(2,1)}) %all-gather.6.cloned.1.call-update) | async-done | bytes 1441808 | tf_op jit(solution)/shard_map/all_gather | solution.py:25
  47.0 1.5 copy.22
  49.2 33.3 %all-gather.8.cloned.1.call-done = bf16[1,352,2048]{2,1,0:T(8,128)(2,1)} async-done(((bf16[1,352,512]{2,1,0:T(8,128)(2,1)}), bf16[1,352,2048]{2,1,0:T(8,128)(2,1)}) %all-gather.8.cloned.1.call-update) | async-done | bytes 1441808 | tf_op jit(solution)/shard_map/all_gather | solution.py:26
  82.5 1.9 fusion.18
  84.4 33.4 %all-gather.10.cloned.1.call-done = bf16[1,352,2048]{2,1,0:T(8,128)(2,1)} async-done(((bf16[1,352,512]{2,1,0:T(8,128)(2,1)}), bf16[1,352,2048]{2,1,0:T(8,128)(2,1)}) %all-gather.10.cloned.1.call-update) | async-done | bytes 1441808 | tf_op jit(solution)/shard_map/all_gather | solution.py:27
  117.8 1.7 convolution_convert_fusion.1
  119.5 0.8 reshape.560
  120.3 3.4 %all-to-all-start.1 = ((bf16[4,12,2048]{2,1,0:T(8,128)(2,1)}), bf16[4,12,2048]{2,1,0:T(8,128)(2,1)S(1)}, u32[]{:S(2)}, u32[]{:S(2)}) async-start(bf16[4,12,2048]{2,1,0:T(8,128)(2,1)} %reshape.560), calls=%async_computation.1 | async-start | bytes 524288 | tf_op jit(solution)/shard_map/all_to_all | solution.py:100
  123.9 5.8 %all-to-all-done.1 = bf16[4,12,2048]{2,1,0:T(8,128)(2,1)S(1)} async-done(((bf16[4,12,2048]{2,1,0:T(8,128)(2,1)}), bf16[4,12,2048]{2,1,0:T(8,128)(2,1)S(1)}, u32[]{:S(2)}, u32[]{:S(2)}) %all-to-all-start.1) | async-done | bytes 196640 | tf_op jit(solution)/shard_map/all_to_all | solution.py:100
  130.3 3.2 %all-to-all-start.4 = ((bf16[4,1,12]{2,1,0:T(2,128)(2,1)}), bf16[4,1,12]{2,1,0:T(2,128)(2,1)S(1)}, u32[]{:S(2)}, u32[]{:S(2)}) async-start(bf16[4,1,12]{2,1,0:T(2,128)(2,1)} %reshape.565), calls=%async_computation.4 | async-start | bytes 4096 | tf_op jit(solution)/shard_map/all_to_all | solution.py:77
  134.2 3.0 %all-to-all-done.4 = bf16[4,1,12]{2,1,0:T(2,128)(2,1)S(1)} async-done(((bf16[4,1,12]{2,1,0:T(2,128)(2,1)}), bf16[4,1,12]{2,1,0:T(2,128)(2,1)S(1)}, u32[]{:S(2)}, u32[]{:S(2)}) %all-to-all-start.4) | async-done | bytes 128 | tf_op jit(solution)/shard_map/all_to_all | solution.py:77
  137.8 3.2 %all-to-all-start.6 = ((bf16[4,1,12]{2,1,0:T(2,128)(2,1)}), bf16[4,1,12]{2,1,0:T(2,128)(2,1)S(1)}, u32[]{:S(2)}, u32[]{:S(2)}) async-start(bf16[4,1,12]{2,1,0:T(2,128)(2,1)} %reshape.568), calls=%async_computation.6 | async-start | bytes 4096 | tf_op jit(solution)/shard_map/all_to_all | solution.py:77
  141.0 4.2 %collective-permute-start = (bf16[64,2048]{1,0:T(8,128)(2,1)S(1)}, bf16[64,2048]{1,0:T(8,128)(2,1)}, u32[]{:S(2)}, u32[]{:S(2)}) collective-permute-start(bf16[64,2048]{1,0:T(8,128)(2,1)S(1)} %fusion), channel_id=1, source_target_pairs={{0,16},{1,17},{2,18},{3,19},{4,20},{5,21},{6,22},{7,23},{8,24},{9,... | collective-permute-start | bytes 786440 | tf_op jit(solution)/shard_map/ppermute | solution.py:13
  145.2 0.7 reshape.566
  145.9 3.4 %all-to-all-start.5 = ((bf16[4,12,2048]{2,1,0:T(8,128)(2,1)}), bf16[4,12,2048]{2,1,0:T(8,128)(2,1)S(1)}, u32[]{:S(2)}, u32[]{:S(2)}) async-start(bf16[4,12,2048]{2,1,0:T(8,128)(2,1)} %reshape.566), calls=%async_computation.5 | async-start | bytes 524288 | tf_op jit(solution)/shard_map/all_to_all | solution.py:76
  149.5 5.8 %all-to-all-done.5 = bf16[4,12,2048]{2,1,0:T(8,128)(2,1)S(1)} async-done(((bf16[4,12,2048]{2,1,0:T(8,128)(2,1)}), bf16[4,12,2048]{2,1,0:T(8,128)(2,1)S(1)}, u32[]{:S(2)}, u32[]{:S(2)}) %all-to-all-start.5) | async-done | bytes 196640 | tf_op jit(solution)/shard_map/all_to_all | solution.py:76
  156.0 3.4 %all-to-all-start.7 = ((bf16[4,12,2048]{2,1,0:T(8,128)(2,1)}), bf16[4,12,2048]{2,1,0:T(8,128)(2,1)S(1)}, u32[]{:S(2)}, u32[]{:S(2)}) async-start(bf16[4,12,2048]{2,1,0:T(8,128)(2,1)} %reshape.569), calls=%async_computation.7 | async-start | bytes 524288 | tf_op jit(solution)/shard_map/all_to_all | solution.py:76
  160.2 5.2 %all-to-all-done.7 = bf16[4,12,2048]{2,1,0:T(8,128)(2,1)S(1)} async-done(((bf16[4,12,2048]{2,1,0:T(8,128)(2,1)}), bf16[4,12,2048]{2,1,0:T(8,128)(2,1)S(1)}, u32[]{:S(2)}, u32[]{:S(2)}) %all-to-all-start.7) | async-done | bytes 196640 | tf_op jit(solution)/shard_map/all_to_all | solution.py:76
  166.7 0.7 reshape.562
  167.4 3.4 %all-to-all-start.2 = ((bf16[4,12,2048]{2,1,0:T(8,128)(2,1)}), bf16[4,12,2048]{2,1,0:T(8,128)(2,1)S(1)}, u32[]{:S(2)}, u32[]{:S(2)}) async-start(bf16[4,12,2048]{2,1,0:T(8,128)(2,1)} %reshape.562), calls=%async_computation.2 | async-start | bytes 524288 | tf_op jit(solution)/shard_map/all_to_all | solution.py:75
  170.9 3.1 %fusion.39 = f32[352,2048]{1,0:T(8,128)} fusion(bf16[48,2048]{1,0:T(8,128)(2,1)S(1)} %reshape.567, bf16[48,352]{1,0:T(8,128)(2,1)} %copy-done.9, f32[48]{0:T(128)S(1)} %reshape.574), kind=kOutput, calls=%fused_computation.48 | convolution fusion | flops 69256704 | bytes 3114176 | tf_op jit(solution)/shard_map/dot_general | solution.py:95
  174.0 2.8 %all-to-all-done.2 = bf16[4,12,2048]{2,1,0:T(8,128)(2,1)S(1)} async-done(((bf16[4,12,2048]{2,1,0:T(8,128)(2,1)}), bf16[4,12,2048]{2,1,0:T(8,128)(2,1)S(1)}, u32[]{:S(2)}, u32[]{:S(2)}) %all-to-all-start.2) | async-done | bytes 196640 | tf_op jit(solution)/shard_map/all_to_all | solution.py:75
  178.7 2.2 convolution_add_fusion
  180.9 1.3 copy-done.1
  182.6 8.4 %all_to_all.42 = bf16[4,12,2048]{2,1,0:T(8,128)(2,1)S(1)} all-to-all(bf16[4,12,2048]{2,1,0:T(8,128)(2,1)S(1)} %reshape.564), channel_id=1, replica_groups=mesh['section'=2,'expert'=4,'dp'=4] {'expert'}, dimensions={0} | all-to-all | bytes 393216 | tf_op jit(solution)/shard_map/all_to_all | solution.py:100
  191.8 0.8 maximum_bitcast_fusion
  192.6 43.3 %reduce-scatter.2.cloned.1.call-done = f32[352,512]{1,0:T(8,128)} async-done(((f32[352,2048]{1,0:T(8,128)}), f32[352,512]{1,0:T(8,128)}) %reduce-scatter.2.cloned.1.call-update) | async-done | bytes 720912 | tf_op jit(solution)/shard_map/reduce_scatter | solution.py:109
  (81 shorter events, 11.9 us)
Async XLA Ops:
  7.2 10.1 %copy-start.11 = (s32[1,2,64,6]{2,1,3,0:T(2,128)S(1)}, s32[1,2,64,6]{2,1,3,0:T(2,128)}, u32[]{:S(2)}) copy-start(s32[1,2,64,6]{2,1,3,0:T(2,128)} %param.11) | copy-start | bytes 9220
  7.2 4.5 %copy-start.3 = (bf16[1,64,2048]{2,1,0:T(8,128)(2,1)S(1)}, bf16[1,64,2048]{2,1,0:T(8,128)(2,1)}, u32[]{:S(2)}) copy-start(bf16[1,64,2048]{2,1,0:T(8,128)(2,1)} %param.9) | copy-start | bytes 786436
  7.2 4.5 %copy-start.14 = (f32[1,2048]{1,0:T(1,128)S(1)}, f32[1,2048]{1,0:T(1,128)}, u32[]{:S(2)}) copy-start(f32[1,2048]{1,0:T(1,128)} %param.14) | copy-start | bytes 24580
  7.2 10.1 %copy-start.12 = (bf16[1,2,64,6]{2,1,3,0:T(2,128)(2,1)S(1)}, bf16[1,2,64,6]{2,1,3,0:T(2,128)(2,1)}, u32[]{:S(2)}) copy-start(bf16[1,2,64,6]{2,1,3,0:T(2,128)(2,1)} %param.12) | copy-start | bytes 4612
  7.2 39.8 %all-gather.6.cloned.1.call-start = ((), (), s32[]{:S(2)}) async-start(), calls=%async_computation.9 | async-start | bytes 1802240 | tf_op jit(solution)/shard_map/all_gather | solution.py:25
  7.9 74.5 %all-gather.8.cloned.1.call-start = ((), (), s32[]{:S(2)}) async-start(), calls=%async_computation.11 | async-start | bytes 1802240 | tf_op jit(solution)/shard_map/all_gather | solution.py:26
  8.7 109.1 %all-gather.10.cloned.1.call-start = ((), (), s32[]{:S(2)}) async-start(), calls=%async_computation.12 | async-start | bytes 1802240 | tf_op jit(solution)/shard_map/all_gather | solution.py:27
  12.7 10.3 %all-to-all-start = ((bf16[4,12,2048]{2,1,0:T(8,128)(2,1)}), bf16[4,12,2048]{2,1,0:T(8,128)(2,1)S(1)}, u32[]{:S(2)}, u32[]{:S(2)}) async-start(bf16[4,12,2048]{2,1,0:T(8,128)(2,1)} %reshape.556), calls=%async_computation | async-start | bytes 524288 | tf_op jit(solution)/shard_map/all_to_all | solution.py:75
  84.4 35.9 %copy-start.9 = (bf16[48,352]{1,0:T(8,128)(2,1)}, bf16[48,352]{1,0:T(8,128)(2,1)S(1)}, u32[]{:S(2)}) copy-start(bf16[48,352]{1,0:T(8,128)(2,1)S(1)} %fusion.18) | copy-start | bytes 101380
  84.4 39.3 %copy-start.8 = (bf16[1,2,64,2048]{3,2,1,0:T(8,128)(2,1)S(1)}, bf16[1,2,64,2048]{3,2,1,0:T(8,128)(2,1)}, u32[]{:S(2)}) copy-start(bf16[1,2,64,2048]{3,2,1,0:T(8,128)(2,1)} %param.13) | copy-start | bytes 1572868
  120.3 9.4 %all-to-all-start.1 = ((bf16[4,12,2048]{2,1,0:T(8,128)(2,1)}), bf16[4,12,2048]{2,1,0:T(8,128)(2,1)S(1)}, u32[]{:S(2)}, u32[]{:S(2)}) async-start(bf16[4,12,2048]{2,1,0:T(8,128)(2,1)} %reshape.560), calls=%async_computation.1 | async-start | bytes 524288 | tf_op jit(solution)/shard_map/all_to_all | solution.py:100
  130.3 6.9 %all-to-all-start.4 = ((bf16[4,1,12]{2,1,0:T(2,128)(2,1)}), bf16[4,1,12]{2,1,0:T(2,128)(2,1)S(1)}, u32[]{:S(2)}, u32[]{:S(2)}) async-start(bf16[4,1,12]{2,1,0:T(2,128)(2,1)} %reshape.565), calls=%async_computation.4 | async-start | bytes 4096 | tf_op jit(solution)/shard_map/all_to_all | solution.py:77
  134.2 31.3 %copy-start.6 = (bf16[64,2048]{1,0:T(8,128)(2,1)}, bf16[64,2048]{1,0:T(8,128)(2,1)S(1)}, u32[]{:S(2)}) copy-start(bf16[64,2048]{1,0:T(8,128)(2,1)S(1)} %fusion) | copy-start | bytes 786436
  137.8 7.4 %all-to-all-start.6 = ((bf16[4,1,12]{2,1,0:T(2,128)(2,1)}), bf16[4,1,12]{2,1,0:T(2,128)(2,1)S(1)}, u32[]{:S(2)}, u32[]{:S(2)}) async-start(bf16[4,1,12]{2,1,0:T(2,128)(2,1)} %reshape.568), calls=%async_computation.6 | async-start | bytes 4096 | tf_op jit(solution)/shard_map/all_to_all | solution.py:77
  141.0 24.5 %copy-start.10 = (bf16[1,64,2048]{2,1,0:T(8,128)(2,1)S(1)}, bf16[1,64,2048]{2,1,0:T(8,128)(2,1)}, u32[]{:S(2)}) copy-start(bf16[1,64,2048]{2,1,0:T(8,128)(2,1)} %param.10) | copy-start | bytes 786436
  141.0 24.5 %collective-permute-start = (bf16[64,2048]{1,0:T(8,128)(2,1)S(1)}, bf16[64,2048]{1,0:T(8,128)(2,1)}, u32[]{:S(2)}, u32[]{:S(2)}) collective-permute-start(bf16[64,2048]{1,0:T(8,128)(2,1)S(1)} %fusion), channel_id=1, source_target_pairs={{0,16},{1,17},{2,18},{3,19},{4,20},{5,21},{6,22},{7,23},{8,24},{9,... | collective-permute-start | bytes 786440 | tf_op jit(solution)/shard_map/ppermute | solution.py:13
  145.9 9.4 %all-to-all-start.5 = ((bf16[4,12,2048]{2,1,0:T(8,128)(2,1)}), bf16[4,12,2048]{2,1,0:T(8,128)(2,1)S(1)}, u32[]{:S(2)}, u32[]{:S(2)}) async-start(bf16[4,12,2048]{2,1,0:T(8,128)(2,1)} %reshape.566), calls=%async_computation.5 | async-start | bytes 524288 | tf_op jit(solution)/shard_map/all_to_all | solution.py:76
  156.0 9.4 %all-to-all-start.7 = ((bf16[4,12,2048]{2,1,0:T(8,128)(2,1)}), bf16[4,12,2048]{2,1,0:T(8,128)(2,1)S(1)}, u32[]{:S(2)}, u32[]{:S(2)}) async-start(bf16[4,12,2048]{2,1,0:T(8,128)(2,1)} %reshape.569), calls=%async_computation.7 | async-start | bytes 524288 | tf_op jit(solution)/shard_map/all_to_all | solution.py:76
  165.7 0.7 copy-start.4
  167.4 9.4 %all-to-all-start.2 = ((bf16[4,12,2048]{2,1,0:T(8,128)(2,1)}), bf16[4,12,2048]{2,1,0:T(8,128)(2,1)S(1)}, u32[]{:S(2)}, u32[]{:S(2)}) async-start(bf16[4,12,2048]{2,1,0:T(8,128)(2,1)} %reshape.562), calls=%async_computation.2 | async-start | bytes 524288 | tf_op jit(solution)/shard_map/all_to_all | solution.py:75
  170.8 65.0 %reduce-scatter.2.cloned.1.call-start = ((), (), s32[]{:S(2)}) async-start(), calls=%async_computation.10 | async-start | bytes 3604480 | tf_op jit(solution)/shard_map/reduce_scatter | solution.py:109
  170.9 6.6 %copy-start.2 = (bf16[1,352,2048]{2,1,0:T(8,128)(2,1)S(1)}, bf16[1,352,2048]{2,1,0:T(8,128)(2,1)}, u32[]{:S(2)}) copy-start(bf16[1,352,2048]{2,1,0:T(8,128)(2,1)} %all-gather.8.cloned.1.call-done) | copy-start | bytes 4325380
  176.8 1.8 copy-start
  176.8 1.8 copy-start.13
  180.9 1.4 copy-start.1
  182.2 8.9 %copy-start.5 = (bf16[64,2048]{1,0:T(8,128)(2,1)S(1)}, bf16[64,2048]{1,0:T(8,128)(2,1)}, u32[]{:S(2)}) copy-start(bf16[64,2048]{1,0:T(8,128)(2,1)} %copy-done.4) | copy-start | bytes 786436
  182.2 9.5 %copy-start.7 = (bf16[64,2048]{1,0:T(8,128)(2,1)S(1)}, bf16[64,2048]{1,0:T(8,128)(2,1)}, u32[]{:S(2)}) copy-start(bf16[64,2048]{1,0:T(8,128)(2,1)} %copy-done.6) | copy-start | bytes 786436
Sparse Core Ops, SparseCore 0:
  9.6 37.4 all-gather.5
  48.6 33.8 all-gather.7
  84.0 33.7 all-gather.9
  181.0 54.8 reduce-scatter.1
